TPU v7x, 32 devices: a whole 2x2x4 slice. The times are simulated.
32 devices in a mesh: kpt: 2 (over x), row: 8 (over z, y), col: 2 (over core).
Axes of the slice: x: 2, y: 2, z: 4, core: 2. Of those that a mesh axis runs over, the one named last changes fastest.
Arguments:
- wannier: float32 [64, 32, 1024], P('kpt', ('row', 'col')), parts along dimension 0, may hold values from -6 to 6
- pairs: int32 [384, 2], replicated, may hold values from 0 to 31, as said below
- gmap: int32 [8192], replicated, may hold values from 1 to 32767, as said below
- screened: bfloat16 [4, 2, 8192, 8192], P('kpt', None, 'row', 'col'), parts along dimension 0, may hold values from -0.046875 to 0.046875
Outputs:
- coulomb: float32 [2, 2, 768, 384], P(None, None, ('kpt', 'row', 'col')), parts along dimension 2
There are 2 independent parts, one for each index of `kpt`. A program takes and returns all parts, laid end to end along the dimension named above; an argument that names none is the same for every part. Nothing has to cross between parts.
Inputs may be any that keep to these rules, and one draw needn't show every extreme that they name: `gmap`: 8192 distinct flat cells of the grid; cell 0 is never among them. `pairs`: in each row the first Wannier function is no greater than the second; no two rows are equal.
All inputs are finite; a program needn't handle non-finite values.
Results may differ from a plain program's by a relative error of at most 0.0082.
Values may be sent and summed in bfloat16 or wider, within the bound.
A program may use at most 128 MiB of HBM per device.

v0:
```python
import math

import jax
import jax.numpy as jnp
from jax import lax
from jax.sharding import PartitionSpec as P

NW = 32
GX = 32
NG = 8192
NP = 384


def line_tables(side_len):
    positions = jnp.arange(side_len, dtype=jnp.int32)
    phase_index = positions[:, None] * positions[None, :] % side_len
    angles = phase_index.astype(jnp.float32) * (2.0 * math.pi / side_len)
    return (jnp.cos(angles), jnp.sin(angles))


def plane_transform(density):
    cosine, sine_table = line_tables(GX)
    highest = lax.Precision.HIGHEST
    shaped = density.reshape(-1, GX, GX)
    real_z = jnp.einsum("nyz,kz->nyk", shaped, cosine, precision=highest)
    imag_z = -jnp.einsum("nyz,kz->nyk", shaped, sine_table, precision=highest)
    new_real = jnp.einsum("jy,nyk->njk", cosine, real_z, precision=highest) + jnp.einsum(
        "jy,nyk->njk", sine_table, imag_z, precision=highest
    )
    new_imag = jnp.einsum("jy,nyk->njk", cosine, imag_z, precision=highest) - jnp.einsum(
        "jy,nyk->njk", sine_table, real_z, precision=highest
    )
    return (new_real.reshape(density.shape), new_imag.reshape(density.shape))


def line_transform(real_part, imag_part):
    cosine, sine_table = line_tables(GX)
    highest = lax.Precision.HIGHEST
    new_real = jnp.einsum("kn,pny->pky", cosine, real_part, precision=highest) + jnp.einsum(
        "kn,pny->pky", sine_table, imag_part, precision=highest
    )
    new_imag = jnp.einsum("kn,pny->pky", cosine, imag_part, precision=highest) - jnp.einsum(
        "kn,pny->pky", sine_table, real_part, precision=highest
    )
    return (new_real, new_imag)


def right_columns(screened, segment):
    w_real = screened[:, 0]
    w_imag = screened[:, 1]
    real_real = jnp.einsum("fgh,bh->fgb", w_real, segment[0], preferred_element_type=jnp.float32)
    imag_imag = jnp.einsum("fgh,bh->fgb", w_imag, segment[1], preferred_element_type=jnp.float32)
    real_imag = jnp.einsum("fgh,bh->fgb", w_real, segment[1], preferred_element_type=jnp.float32)
    imag_real = jnp.einsum("fgh,bh->fgb", w_imag, segment[0], preferred_element_type=jnp.float32)
    return jnp.stack([real_real - imag_imag, real_imag + imag_real], axis=1)


def shards(wannier, pairs, gmap, screened):
    planes = wannier.shape[1]
    grid_cells = wannier.shape[2]
    members = jnp.arange(NW, dtype=jnp.int32)[None, :]
    pick_first = (pairs[:, 0:1] == members).astype(jnp.float32)
    pick_second = (pairs[:, 1:2] == members).astype(jnp.float32)
    flat_rows = wannier.reshape(NW, -1)
    highest = lax.Precision.HIGHEST
    density = jnp.dot(pick_first, flat_rows, precision=highest) * jnp.dot(
        pick_second, flat_rows, precision=highest
    )
    density = density.reshape(NP, planes, grid_cells)
    arrived = lax.all_to_all(density, ("row", "col"), split_axis=0, concat_axis=1, tiled=True)
    real_part, imag_part = plane_transform(arrived)
    real_part, imag_part = line_transform(real_part, imag_part)
    owned = real_part.shape[0]
    norm_factor = 1.0 / math.sqrt(GX * GX * GX)
    rho_real = jnp.take(real_part.reshape(owned, -1), gmap, axis=1) * norm_factor
    rho_imag = jnp.take(imag_part.reshape(owned, -1), gmap, axis=1) * norm_factor
    rho = jnp.stack([rho_real, rho_imag], axis=0).astype(jnp.bfloat16)
    row_span = screened.shape[2]
    halves = lax.all_to_all(rho, "col", split_axis=2, concat_axis=1, tiled=True)
    screened_rho = right_columns(screened, lax.all_gather(halves, "row", axis=1, tiled=True))
    blocks = lax.all_to_all(rho, "row", split_axis=2, concat_axis=1, tiled=True)
    blocks = blocks.reshape(2, lax.axis_size("row"), owned, row_span)
    left_panel = lax.all_gather(blocks, "col", axis=2, tiled=True).reshape(2, NP, row_span)
    left_wide = left_panel.astype(jnp.float32)
    u_real = jnp.einsum(
        "ag,fgb->fab", left_wide[0], screened_rho[:, 0], precision=highest
    ) + jnp.einsum("ag,fgb->fab", left_wide[1], screened_rho[:, 1], precision=highest)
    u_imag = jnp.einsum(
        "ag,fgb->fab", left_wide[0], screened_rho[:, 1], precision=highest
    ) - jnp.einsum("ag,fgb->fab", left_wide[1], screened_rho[:, 0], precision=highest)
    partial_terms = jnp.stack([u_real, u_imag], axis=1) / math.sqrt(NG)
    summed = lax.psum(partial_terms, ("row", "col"))
    share_rows = NP // lax.axis_size(("row", "col"))
    return lax.dynamic_slice_in_dim(
        summed, lax.axis_index(("row", "col")) * share_rows, share_rows, 2
    )


def solution(mesh):
    return jax.shard_map(
        shards,
        mesh=mesh,
        in_specs=(P("kpt", ("row", "col"), None), P(), P(), P("kpt", None, "row", "col")),
        out_specs=P(None, None, ("kpt", "row", "col"), None),
        check_vma=False,
    )
```

profile of v0, /device:TPU:0, one launch (start us, length us, event | category | flops | bytes accessed | tf_op | source)
XLA Modules:
  0.0 687.3 jit_solution(8600309741713015094)
XLA Ops:
  15.1 7.5 %all-to-all-start = ((f32[384,2,1024]{2,1,0:T(2,128)}), f32[384,2,1024]{2,1,0:T(2,128)S(1)}, u32[]{:S(2)}, u32[]{:S(2)}) async-start(f32[384,2,1024]{2,1,0:T(2,128)} %reshape.35), calls=%async_computation | async-start | bytes 6291456 | tf_op jit(solution)/shard_map/all_to_all | solution.py:70
  22.7 59.1 %all-to-all-done = f32[384,2,1024]{2,1,0:T(2,128)S(1)} async-done(((f32[384,2,1024]{2,1,0:T(2,128)}), f32[384,2,1024]{2,1,0:T(2,128)S(1)}, u32[]{:S(2)}, u32[]{:S(2)}) %all-to-all-start) | async-done | bytes 3145760 | tf_op jit(solution)/shard_map/all_to_all | solution.py:70
  85.3 7.6 %reshape.36 = f32[768,32,32]{2,1,0:T(8,128)} reshape(f32[24,16,2,1024]{3,2,1,0:T(2,128)S(1)} %copy.71) | data formatting | bytes 6291456 | tf_op jit(solution)/shard_map/reshape | solution.py:24
  92.9 9.2 %copy.72 = f32[768,32,32]{0,2,1:T(8,128)S(1)} copy(f32[768,32,32]{2,1,0:T(8,128)} %reshape.36) | data formatting | bytes 6291456 | tf_op jit(solution)/shard_map/reshape | solution.py:24
  130.5 10.6 %copy.79 = f32[768,32,32]{2,1,0:T(8,128)} copy(f32[768,32,32]{0,1,2:T(8,128)S(1)} %subtract_bitcast_fusion.1) | data formatting | bytes 6291456 | tf_op jit(solution)/shard_map/sub | solution.py:30
  141.1 9.4 %reshape.38 = f32[24,32,1024]{2,1,0:T(8,128)S(1)} reshape(f32[768,32,32]{2,1,0:T(8,128)} %copy.79) | data formatting | bytes 6291456 | tf_op jit(solution)/shard_map/reshape | solution.py:33
  155.9 11.4 %copy.76 = f32[768,32,32]{2,1,0:T(8,128)} copy(f32[768,32,32]{0,1,2:T(8,128)} %add_bitcast_fusion.1) | data formatting | bytes 6291456 | tf_op jit(solution)/shard_map/add | solution.py:27
  167.3 10.7 %reshape.37 = f32[24,32,1024]{2,1,0:T(8,128)} reshape(f32[768,32,32]{2,1,0:T(8,128)} %copy.76) | data formatting | bytes 6291456 | tf_op jit(solution)/shard_map/reshape | solution.py:33
  195.1 10.3 %copy.89 = f32[24,32,1024]{0,2,1:T(8,128)} copy(f32[24,32,1024]{2,1,0:T(8,128)} %add_bitcast_fusion) | data formatting | bytes 6291456 | tf_op jit(solution)/shard_map/reshape | solution.py:75
  205.4 8.6 %copy.90 = f32[24,32,1024]{0,2,1:T(8,128)} copy(f32[24,32,1024]{2,1,0:T(8,128)S(1)} %copy-done.2) | data formatting | bytes 6291456 | tf_op jit(solution)/shard_map/reshape | solution.py:76
  214.0 33.6 %gather_fusion = f32[8192,24]{1,0:T(8,128)} fusion(f32[24,32768]{0,1:T(8,128)} %bitcast.144, s32[8192]{0:T(1024)S(1)} %fusion.57), kind=kCustom, calls=%fused_computation.clone | custom fusion | bytes 1605632 | tf_op jit(solution)/shard_map/jit(_take)/gather | solution.py:75
  247.6 33.6 %gather_fusion.1 = f32[8192,24]{1,0:T(8,128)} fusion(f32[24,32768]{0,1:T(8,128)} %bitcast.143, s32[8192]{0:T(1024)S(1)} %fusion.57), kind=kCustom, calls=%fused_computation.1.clone | custom fusion | bytes 1605632 | tf_op jit(solution)/shard_map/jit(_take)/gather | solution.py:76
  289.4 35.5 %copy.108 = bf16[2,24,8192]{1,0,2:T(2,128)(2,1)} copy(bf16[2,24,8192]{1,2,0:T(8,128)(2,1)S(1)} %pad_maximum_fusion) | data formatting | bytes 1572864 | tf_op jit(solution)/shard_map/stack | solution.py:77
  331.5 35.8 %all_to_all.48 = bf16[8,2,24576]{2,1,0:T(2,128)(2,1)S(1)} all-to-all(bf16[8,2,24576]{2,1,0:T(2,128)(2,1)S(1)} %reshape.71), channel_id=1, replica_groups=mesh['kpt'=2,'row'=8,'col'=2] {'row'}, dimensions={0} | all-to-all | bytes 1572864 | tf_op jit(solution)/shard_map/all_to_all | solution.py:81
  374.3 10.3 %copy.87 = bf16[2,24,8,1024]{3,1,2,0:T(8,128)(2,1)} copy(bf16[2,24,8,1024]{1,0,3,2:T(2,128)(2,1)} %bitcast.145) | data formatting | bytes 1572864 | tf_op jit(solution)/shard_map/all_to_all | solution.py:81
  384.6 10.2 %copy.109 = bf16[2,24,8192]{1,0,2:T(2,128)(2,1)} copy(bf16[2,24,8192]{1,2,0:T(8,128)(2,1)} %copy-done) | data formatting | bytes 1572864 | tf_op jit(solution)/shard_map/stack | solution.py:77
  406.2 7.3 %reshape.74 = bf16[8192,2,24]{2,1,0:T(2,128)(2,1)} reshape(bf16[2,2,98304]{2,1,0:T(2,128)(2,1)S(1)} %all_to_all.49) | data formatting | bytes 1572864
  413.6 9.5 %copy.83 = bf16[2,24,2,4096]{3,1,2,0:T(8,128)(2,1)} copy(bf16[2,24,2,4096]{1,0,3,2:T(2,128)(2,1)} %bitcast.146) | data formatting | bytes 1572864 | tf_op jit(solution)/shard_map/all_to_all | solution.py:79
  424.7 96.3 %all-gather.3.cloned.1.call-done = bf16[2,384,4096]{2,1,0:T(8,128)(2,1)} async-done(((bf16[2,48,4096]{2,1,0:T(8,128)(2,1)}), bf16[2,384,4096]{2,1,0:T(8,128)(2,1)}) %all-gather.3.cloned.1.call-update) | async-done | bytes 6291472 | tf_op jit(solution)/shard_map/all_gather | solution.py:80
  521.0 11.4 %fusion = f32[384,2,1024]{2,0,1:T(8,128)S(1)} fusion(bf16[2,2,1024,4096]{3,2,1,0:T(8,128)(2,1)} %param.9, bf16[2,384,4096]{2,1,0:T(8,128)(2,1)} %all-gather.3.cloned.1.call-done), kind=kOutput, calls=%fused_computation.2 | convolution fusion | flops 6442450944 | bytes 23068672 | tf_op jit(solution)/shard_map/fgh,bh->fgb/dot_general | solution.py:54
  532.4 11.2 %fusion.39 = f32[384,2,1024]{2,0,1:T(8,128)S(1)} fusion(f32[384,2,1024]{2,0,1:T(8,128)S(1)} %fusion, bf16[2,2,1024,4096]{3,2,1,0:T(8,128)(2,1)} %param.9, bf16[2,384,4096]{2,1,0:T(8,128)(2,1)} %all-gather.3.cloned.1.call-done), kind=kOutput, calls=%fused_computation.47 | convolution fusion | flops 6443237376 | bytes 26214400 | tf_op jit(solution)/shard_map/fgh,bh->fgb/dot_general | solution.py:53
  548.9 12.6 %fusion.2 = f32[384,2,1024]{2,0,1:T(8,128)} fusion(bf16[2,2,1024,4096]{3,2,1,0:T(8,128)(2,1)} %param.9, bf16[2,384,4096]{2,1,0:T(8,128)(2,1)} %all-gather.3.cloned.1.call-done), kind=kOutput, calls=%fused_computation.4 | convolution fusion | flops 6442450944 | bytes 23068672 | tf_op jit(solution)/shard_map/fgh,bh->fgb/dot_general | solution.py:52
  561.5 12.1 %fusion.36 = f32[384,2,1024]{2,0,1:T(8,128)S(1)} fusion(f32[384,2,1024]{2,0,1:T(8,128)} %fusion.2, bf16[2,2,1024,4096]{3,2,1,0:T(8,128)(2,1)} %param.9, bf16[2,384,4096]{2,1,0:T(8,128)(2,1)} %all-gather.3.cloned.1.call-done), kind=kOutput, calls=%fused_computation.46 | convolution fusion | flops 6443237376 | bytes 26214400 | tf_op jit(solution)/shard_map/fgh,bh->fgb/dot_general | solution.py:51
  580.6 97.4 %all-reduce.2.cloned.1.call-done = f32[2,2,384,384]{2,3,0,1:T(8,128)} async-done(((f32[2,2,384,384]{2,3,0,1:T(8,128)}), f32[2,2,384,384]{2,3,0,1:T(8,128)}) %all-reduce.2.cloned.1.call-update) | async-done | bytes 2359312 | tf_op jit(solution)/shard_map/psum | solution.py:92
  (50 shorter events, 112.5 us)
Async XLA Ops:
  15.1 7.6 %copy-start.4 = (s32[8192]{0:T(1024)S(1)}, s32[8192]{0:T(1024)}, u32[]{:S(2)}) copy-start(s32[8192]{0:T(1024)} %param.8) | copy-start | bytes 98308
  15.1 66.8 %all-to-all-start = ((f32[384,2,1024]{2,1,0:T(2,128)}), f32[384,2,1024]{2,1,0:T(2,128)S(1)}, u32[]{:S(2)}, u32[]{:S(2)}) async-start(f32[384,2,1024]{2,1,0:T(2,128)} %reshape.35), calls=%async_computation | async-start | bytes 6291456 | tf_op jit(solution)/shard_map/all_to_all | solution.py:70
  22.6 400.5 %all-gather.5.cloned.1.call-start = ((), (), s32[]{:S(2)}) async-start(), calls=%async_computation.4 | async-start | bytes 2359296 | tf_op jit(solution)/shard_map/all_gather | solution.py:83
  178.0 6.0 copy-start.1
  178.0 6.0 copy-start.3
  195.1 10.3 %copy-start.2 = (f32[24,32,1024]{2,1,0:T(8,128)S(1)}, f32[24,32,1024]{2,1,0:T(8,128)}, u32[]{:S(2)}) copy-start(f32[24,32,1024]{2,1,0:T(8,128)} %subtract_bitcast_fusion) | copy-start | bytes 9437188
  289.4 35.5 %copy-start = (bf16[2,24,8192]{1,2,0:T(8,128)(2,1)}, bf16[2,24,8192]{1,2,0:T(8,128)(2,1)S(1)}, u32[]{:S(2)}) copy-start(bf16[2,24,8192]{1,2,0:T(8,128)(2,1)S(1)} %pad_maximum_fusion) | copy-start | bytes 2359300
  384.6 136.4 %all-gather.3.cloned.1.call-start = ((), (), s32[]{:S(2)}) async-start(), calls=%async_computation.3 | async-start | bytes 7077888 | tf_op jit(solution)/shard_map/all_gather | solution.py:80
  423.1 254.9 %all-reduce.2.cloned.1.call-start = ((), (), s32[]{:S(2)}) async-start(), calls=%async_computation.5 | async-start | bytes 4718592 | tf_op jit(solution)/shard_map/psum | solution.py:92
Sparse Core Ops, SparseCore 0:
  384.7 8.8 all-gather.4
  423.2 97.7 all-gather.2
  580.7 97.1 all-reduce.1
where the time goes:
time: 696 us; the launch traced here: 687 us
  waiting for transfers between devices  253 us (36%)
  local copies, waits for them, and re-layouts  251 us (36%)
  matrix products  112 us (16%)
  blocking collectives  40.1 us (6%)
  between operations  13.7 us (2%)
  other arithmetic  9.75 us (1%)
  starting transfers between devices  7.67 us (1%)
    psum x1, waiting for transfers between devices, shards(): summed = lax.psum(partial_terms, ('row', 'col'))  97.4 us
    all_gather x1, waiting for transfers between devices, shards(): lax.all_gather(halves, 'row', axis=1, tiled=True)  96.3 us
    all_to_all x1, waiting for transfers between devices, shards(): lax.all_to_all(density, ('row', 'col'), split_axis=0, concat_axis=1, tile...  59.1 us
    another operation x2, local copies, waits for them, and re-layouts, shards(): rho = jnp.stack([rho_real, rho_imag], axis=0).astype(jnp.bfloat16)  45.7 us
    all_to_all x1, blocking collectives, shards(): blocks = lax.all_to_all(rho, 'row', split_axis=2, concat_axis=1, tiled=True)  35.8 us
    gather x1, local copies, waits for them, and re-layouts, shards(): jnp.take(imag_part.reshape(owned, -1), gmap, axis=1) * norm_factor  33.6 us
    gather x1, local copies, waits for them, and re-layouts, shards(): jnp.take(real_part.reshape(owned, -1), gmap, axis=1) * norm_factor  33.6 us
    unnamed x15, local copies, waits for them, and re-layouts  29 us
  transfers between devices with their start and end apart: 4, of which 3 were waited for; matrix products, arithmetic and copies ran while one was open for 5% of the time, Pallas kernels for 0%

commit v1 on v0

v1 whole, which is shorter than its diff:
```python
import functools
import math

import jax
import jax.numpy as jnp
from jax import lax
from jax.experimental import pallas as pl
from jax.experimental.pallas import tpu as pltpu
from jax.sharding import PartitionSpec as P

IM = 64
LANES = 128


def twiddle(re, im, c, s):
    if s == 0.0:
        return re, im
    if im is None:
        return re * c, re * (-s)
    if c == 0.0:
        return im * s, re * (-s)
    return re * c + im * s, im * c - re * s


def real_dft(xs):
    n = len(xs)
    if n == 1:
        return [(xs[0], None)]
    if n == 2:
        return [(xs[0] + xs[1], None), (xs[0] - xs[1], None)]
    even, odd = real_dft(xs[0::2]), real_dft(xs[1::2])
    out = [None] * (n // 2 + 1)
    for k in range(n // 4 + 1):
        er, ei = even[k]
        if 4 * k == n:
            c, s = 0.0, 1.0
        elif k == 0:
            c, s = 1.0, 0.0
        else:
            c, s = math.cos(2 * math.pi * k / n), math.sin(2 * math.pi * k / n)
        if c == 0.0 and odd[k][1] is None:
            tr, ti = None, odd[k][0] * -1.0
        else:
            tr, ti = twiddle(odd[k][0], odd[k][1], c, s)
        hi_r = er if tr is None else er + tr
        lo_r = er if tr is None else er - tr
        if ei is None and ti is None:
            hi_i = lo_i = None
        elif ei is None:
            hi_i, lo_i = ti, ti
        elif ti is None:
            hi_i, lo_i = ei, -ei
        else:
            hi_i, lo_i = ei + ti, ti - ei
        out[k] = (hi_r, hi_i)
        if n // 2 - k != k:
            out[n // 2 - k] = (lo_r, lo_i)
    return out


def rho_kernel(norm, index_ref, sel_ref, grid_ref, table_ref, sign_ref, out_ref, dens, spec, cells, rows):
    planes, _, area = grid_ref.shape
    padded = sel_ref.shape[0] // 2
    half = planes // 2 + 1
    groups = spec.shape[0] // 2

    def plane(x, carry):
        both = jnp.dot(sel_ref[...], grid_ref[x], preferred_element_type=jnp.float32)
        dens[x] = both[:padded] * both[padded:]
        return carry

    lax.fori_loop(0, planes, plane, 0)
    for k in range(spec.shape[0]):
        if k >= half:
            spec[k] = jnp.zeros(spec.shape[1:], spec.dtype)
        else:
            if padded < IM:
                pad = jnp.zeros((IM - padded, 2 * area), spec.dtype)
                spec[k, padded:IM] = pad
                spec[k, IM + padded :] = pad

    def chunk(i, carry):
        p0 = pl.multiple_of((i // (area // LANES)) * 16, 16)
        n0 = pl.multiple_of((i % (area // LANES)) * LANES, LANES)
        n1 = pl.multiple_of(n0 + area, LANES)
        p1 = pl.multiple_of(p0 + IM, 16)
        terms = [dens[x, pl.ds(p0, 16), pl.ds(n0, LANES)] for x in range(planes)]
        for k, (re, im) in enumerate(real_dft(terms)):
            re = re * norm
            im = jnp.zeros_like(re) if im is None else im * norm
            re_b, im_b = re.astype(jnp.bfloat16), im.astype(jnp.bfloat16)
            spec[k, pl.ds(p0, 16), pl.ds(n0, LANES)] = re_b
            spec[k, pl.ds(p0, 16), pl.ds(n1, LANES)] = im_b
            spec[k, pl.ds(p1, 16), pl.ds(n0, LANES)] = im_b
            spec[k, pl.ds(p1, 16), pl.ds(n1, LANES)] = (-re).astype(jnp.bfloat16)
        return carry

    lax.fori_loop(0, (padded // 16) * (area // LANES), chunk, 0)
    tile = 256
    steps = area // tile

    def product(i, carry):
        k = (i // steps) * 2
        m0 = pl.multiple_of((i % steps) * tile, tile)
        right = spec[pl.ds(k, 2)].reshape(2 * LANES, 2 * area)
        got = lax.dot_general(
            table_ref[pl.ds(m0, tile), :], right, (((1,), (1,)), ((), ())), preferred_element_type=jnp.float32
        )
        first = pl.multiple_of(k * area + m0, tile)
        second = pl.multiple_of(first + area, tile)
        cells[pl.ds(first, tile), :] = got[:, :LANES]
        cells[pl.ds(second, tile), :] = got[:, LANES:]
        return carry

    lax.fori_loop(0, groups * steps, product, 0)
    count = rows.shape[0]
    unroll = 16

    def pick(i, carry):
        base = pl.multiple_of(i * unroll, unroll)
        for j in range(unroll):
            rows[pl.ds(base + j, 1), :] = cells[pl.ds(index_ref[base + j], 1), :]
        return carry

    lax.fori_loop(0, count // unroll, pick, 0)
    span = 256

    def turn(i, carry):
        g0 = pl.multiple_of(i * span, span)
        flipped = rows[pl.ds(g0, span), :].T
        out_ref[0, :, pl.ds(g0, span)] = flipped[:padded].astype(jnp.bfloat16)
        signed = flipped[IM : IM + padded] * sign_ref[:, pl.ds(g0, span)]
        out_ref[1, :, pl.ds(g0, span)] = signed.astype(jnp.bfloat16)
        return carry

    lax.fori_loop(0, count // span, turn, 0)


def pair_coefficients(grid, table, sel, index, sign):
    planes, _, area = grid.shape
    padded = sel.shape[0] // 2
    count = index.shape[0]
    half = planes // 2 + 1
    even_half = half + half % 2
    norm = 1.0 / math.sqrt(planes * area)
    whole = pl.BlockSpec(memory_space=pltpu.VMEM)
    return pl.pallas_call(
        functools.partial(rho_kernel, norm),
        out_shape=jax.ShapeDtypeStruct((2, padded, count), jnp.bfloat16),
        in_specs=[pl.BlockSpec(memory_space=pltpu.SMEM), whole, whole, whole, whole],
        out_specs=whole,
        scratch_shapes=[
            pltpu.VMEM((planes, padded, area), jnp.float32),
            pltpu.VMEM((even_half, LANES, 2 * area), jnp.bfloat16),
            pltpu.VMEM((even_half * area, LANES), jnp.float32),
            pltpu.VMEM((count, LANES), jnp.float32),
        ],
        compiler_params=pltpu.CompilerParams(vmem_limit_bytes=60 * 1024 * 1024),
        cost_estimate=pl.CostEstimate(flops=10**10, bytes_accessed=8 * 1024 * 1024, transcendentals=0),
        name="rho",
    )(index, sel, grid, table, sign)


def element_kernel(scale, w_ref, right_ref, left_ref, out_ref, right):
    members, parts, owned, _ = right_ref.shape
    pairs = members * owned

    @pl.when((pl.program_id(0) == 0) & (pl.program_id(1) == 0))
    def _():
        for r in range(members):
            for c in range(parts):
                right[c * pairs + r * owned : c * pairs + (r + 1) * owned, :] = right_ref[r, c]

    nt = (((1,), (1,)), ((), ()))
    z_real = lax.dot_general(w_ref[0, 0], right[...], nt, preferred_element_type=jnp.float32)
    z_imag = lax.dot_general(w_ref[0, 1], right[...], nt, preferred_element_type=jnp.float32)
    s_real = (z_real[:, :pairs] - z_imag[:, pairs:]) * scale
    s_imag = (z_real[:, pairs:] + z_imag[:, :pairs]) * scale
    one = jnp.concatenate([s_real, s_imag], axis=1).astype(jnp.bfloat16)
    two = jnp.concatenate([s_imag, -s_real], axis=1).astype(jnp.bfloat16)
    got = jnp.dot(left_ref[0], one, preferred_element_type=jnp.float32)
    got += jnp.dot(left_ref[1], two, preferred_element_type=jnp.float32)

    @pl.when(pl.program_id(1) == 0)
    def _():
        out_ref[0] = got

    @pl.when(pl.program_id(1) > 0)
    def _():
        out_ref[0] += got


def matrix_elements(screened, right, left, scale):
    freqs, parts, rows, columns = screened.shape
    pairs = left.shape[1]
    tile = min(256, rows)
    return pl.pallas_call(
        functools.partial(element_kernel, scale),
        grid=(freqs, rows // tile),
        out_shape=jax.ShapeDtypeStruct((freqs, pairs, parts * pairs), jnp.float32),
        in_specs=[
            pl.BlockSpec((1, parts, tile, columns), lambda f, i: (f, 0, i, 0)),
            pl.BlockSpec(memory_space=pltpu.VMEM),
            pl.BlockSpec((parts, pairs, tile), lambda f, i: (0, 0, i)),
        ],
        out_specs=pl.BlockSpec((1, pairs, parts * pairs), lambda f, i: (f, 0, 0)),
        scratch_shapes=[pltpu.VMEM((parts * pairs, columns), jnp.bfloat16)],
        compiler_params=pltpu.CompilerParams(
            dimension_semantics=("arbitrary", "arbitrary"), vmem_limit_bytes=60 * 1024 * 1024
        ),
        cost_estimate=pl.CostEstimate(
            flops=8 * freqs * rows * columns * pairs, bytes_accessed=2 * screened.size, transcendentals=0
        ),
        name="elements",
    )(screened, right, left)


def plane_table(area):
    side = math.isqrt(area)
    k = lax.broadcasted_iota(jnp.int32, (area, 2 * area), 0)
    n = lax.broadcasted_iota(jnp.int32, (area, 2 * area), 1)
    cell = n % area
    turn = (k // side) * (cell // side) + (k % side) * (cell % side)
    turn = (turn - jnp.where(n >= area, side // 4, 0)) % side
    return jnp.cos(turn.astype(jnp.float32) * (2.0 * math.pi / side)).astype(jnp.bfloat16)


def shards(wannier, pairs, gmap, screened):
    functions, _, area = wannier.shape
    side = math.isqrt(area)
    count = pairs.shape[0]
    members = lax.axis_size("row")
    columns = screened.shape[3]
    row_span = screened.shape[2]
    row, col = lax.axis_index("row"), lax.axis_index("col")
    owned = count // members
    padded = -(-owned // 16) * 16

    local = jnp.swapaxes(wannier, 0, 1).astype(jnp.bfloat16)
    grid = lax.all_gather(local, ("row", "col"), axis=0, tiled=True)
    depth = grid.shape[0]

    mine = lax.dynamic_slice_in_dim(pairs, row * owned, owned, 0)
    mine = jnp.pad(mine, ((0, padded - owned), (0, 0)), constant_values=-1)
    sel = (mine.T.reshape(-1, 1) == jnp.arange(functions, dtype=jnp.int32)[None, :]).astype(jnp.bfloat16)

    flat = lax.dynamic_slice_in_dim(gmap, col * columns, columns, 0)
    kx, ky, kz = flat // area, (flat // side) % side, flat % side
    far = kx > depth // 2
    kx = jnp.where(far, depth - kx, kx)
    ky = jnp.where(far, (side - ky) % side, ky)
    kz = jnp.where(far, (side - kz) % side, kz)
    index = kx * area + ky * side + kz
    sign = jnp.where(far, -1.0, 1.0).astype(jnp.float32)[None, :]

    rho = pair_coefficients(grid, plane_table(area), sel, index, sign)[:, :owned]
    right = lax.all_gather(rho, "row", axis=0, tiled=False)

    start = row * row_span
    block = lax.dynamic_slice_in_dim(right, start % columns, row_span, 3)
    swap = [(i, (i + 1) % lax.axis_size("col")) for i in range(lax.axis_size("col"))]
    other = lax.ppermute(block, "col", swap)
    left = jnp.where(start // columns == col, block, other)
    left = jnp.swapaxes(left, 0, 1).reshape(2, count, row_span)

    partial = matrix_elements(screened, right, left, 1.0 / math.sqrt(gmap.shape[0]))
    freqs = partial.shape[0]
    devices = lax.axis_size(("row", "col"))
    share = count // devices
    pieces = partial.astype(jnp.bfloat16).reshape(freqs, devices, share, 2 * count)
    pieces = jnp.swapaxes(pieces, 0, 1)
    arrived = lax.all_to_all(pieces, ("row", "col"), split_axis=0, concat_axis=0, tiled=True)
    summed = jnp.sum(arrived.astype(jnp.float32), axis=0)
    return summed.reshape(freqs, share, 2, count).transpose(0, 2, 1, 3)


def solution(mesh):
    return jax.shard_map(
        shards,
        mesh=mesh,
        in_specs=(P("kpt", ("row", "col"), None), P(), P(), P("kpt", None, "row", "col")),
        out_specs=P(None, None, ("kpt", "row", "col"), None),
        check_vma=False,
    )
```

time: 696 us -> 276 us (0.40); the launches traced: 687 us -> 276 us
  local copies, waits for them, and re-layouts: 251 us -> 5.59 us
  waiting for transfers between devices: 253 us -> 109 us
  matrix products: 112 us -> 0 us
  Pallas kernels: 0 us -> 74.2 us
  other arithmetic: 9.75 us -> 41.4 us
  blocking collectives: 40.1 us -> 32.2 us
  starting transfers between devices: 7.67 us -> 0.12 us
    dot_general x20 -> x0, matrix products: 112 us -> none  [the longest x1 12.6 us: right_columns(): jnp.einsum('fgh,bh->fgb', w_imag, segment[1], preferred_element_type=jnp....]
    psum x1 -> x0, waiting for transfers between devices: 97.4 us -> none  [shards(): summed = lax.psum(partial_terms, ('row', 'col'))]
    pallas_call x0 -> x2, Pallas kernels: none -> 74.2 us  [the longest x1 38 us: matrix_elements(): pl.pallas_call(functools.partial(element_kernel, scale), grid=(freqs, row...]
    gather x2 -> x0, local copies, waits for them, and re-layouts: 67.3 us -> none  [the longest x1 33.6 us: shards(): jnp.take(imag_part.reshape(owned, -1), gmap, axis=1) * norm_factor]
    reshape x7 -> x2, local copies, waits for them, and re-layouts: 59.4 us -> 0.16 us  [the longest x1 0.08 us: shards(): partial.astype(jnp.bfloat16).reshape(freqs, devices, share, 2 * count)]
    all_to_all x1 -> x0, waiting for transfers between devices: 59.1 us -> none  [shards(): lax.all_to_all(density, ('row', 'col'), split_axis=0, concat_axis=1, tile...]
    another operation x2 -> x0, local copies, waits for them, and re-layouts: 45.7 us -> none  [shards(): rho = jnp.stack([rho_real, rho_imag], axis=0).astype(jnp.bfloat16)]
    convert_element_type x0 -> x3, other arithmetic: none -> 36.4 us  [the longest x1 34 us: plane_table(): jnp.cos(turn.astype(jnp.float32) * (2.0 * math.pi / side))]
  transfers between devices with their start and end apart: 4 -> 3, of which waited for: 3 -> 3; matrix products, arithmetic and copies ran while one was open for 5% -> 14% of each run, Pallas kernels for 0% -> 0%
where the time goes in v1:
time: 276 us
  waiting for transfers between devices  109 us (39%)
  Pallas kernels  74.2 us (27%)
  other arithmetic  41.4 us (15%)
  blocking collectives  32.2 us (12%)
  between operations  13.5 us (5%)
  local copies, waits for them, and re-layouts  5.59 us (2%)
    all_gather x1, waiting for transfers between devices, shards(): right = lax.all_gather(rho, 'row', axis=0, tiled=False)  97.6 us
    pallas_call x1, Pallas kernels, matrix_elements(): pl.pallas_call(functools.partial(element_kernel, scale), grid=(freqs, row...  38 us
    pallas_call x1, Pallas kernels, pair_coefficients(): pl.pallas_call(functools.partial(rho_kernel, norm), out_shape=jax.ShapeDt...  36.3 us
    convert_element_type x1, other arithmetic, plane_table(): jnp.cos(turn.astype(jnp.float32) * (2.0 * math.pi / side))  34 us
    all_to_all x1, blocking collectives, shards(): lax.all_to_all(pieces, ('row', 'col'), split_axis=0, concat_axis=0, tiled...  32.2 us
    all_gather x1, waiting for transfers between devices, shards(): grid = lax.all_gather(local, ('row', 'col'), axis=0, tiled=True)  7.87 us
  transfers between devices with their start and end apart: 3, of which 3 were waited for; matrix products, arithmetic and copies ran while one was open for 14% of the time, Pallas kernels for 0%

profile of v1, /device:TPU:0, one launch (start us, length us, event | category | flops | bytes accessed | tf_op | source)
XLA Modules:
  0.0 276.0 jit_solution(16944760759074681670)
XLA Ops:
  6.5 1.7 copy.19
  8.2 0.0 all-gather.4.cloned.1.call-update
  8.3 0.0 all-gather.6.cloned.1.call-start
  8.3 0.1 dynamic-slice_bitcast_fusion
  8.4 0.1 eq.30
  8.5 1.3 compare_select_fusion
  9.9 1.4 fusion.18.index_ref
  11.2 0.7 fusion.14.sel_ref
  11.9 34.0 %fusion.8.table_ref = bf16[1024,2048]{1,0:T(8,128)(2,1)} fusion(s32[2048]{0:T(1024)S(1)} %fusion.32, s32[1024]{0:T(1024)S(1)} %get-tuple-element.10, s32[1024]{0:T(1024)S(1)} %get-tuple-element.11, s32[2048]{0:T(1024)S(1)} %get-tuple-element.7, s32[2048]{0:T(1024)S(1)} %get-tuple-element.8, s32[1024]{0:T(1024)S(1)} %get-tuple-element.9, ...), kind=kLoop, calls=%fused_computation.19 | loop fusion | flops 83886080 | bytes 4239360 | tf_op jit(solution)/shard_map/convert_element_type | solution.py:225
  45.9 7.9 %all-gather.4.cloned.1.call-done.grid_ref = bf16[32,32,1024]{2,1,0:T(8,128)(2,1)} async-done(((bf16[2,32,1024]{2,1,0:T(8,128)(2,1)}), bf16[32,32,1024]{2,1,0:T(8,128)(2,1)}) %all-gather.4.cloned.1.call-update) | async-done | bytes 2097168 | tf_op jit(solution)/shard_map/all_gather | solution.py:240
  53.8 36.3 %rho.1 = bf16[2,48,4096]{2,1,0:T(8,128)(2,1)} custom-call(s32[4096]{0:T(1024)} %fusion.18.index_ref, bf16[96,32]{1,0:T(8,128)(2,1)} %fusion.14.sel_ref, bf16[32,32,1024]{2,1,0:T(8,128)(2,1)} %all-gather.4.cloned.1.call-done.grid_ref, bf16[1024,2048]{1,0:T(8,128)(2,1)} %fusion.8.table_ref, f32[1,4096]{1,0:T(1,128)} %bitcast.23), custom_call_target="tpu_custom_call" | custom-call | flops 10000000000 | bytes 8388608 | tf_op jit(solution)/shard_map/rho/pallas_call | solution.py:147
  90.1 97.6 %all-gather.6.cloned.1.call-done = bf16[16,48,4096]{2,1,0:T(8,128)(2,1)} async-done(((bf16[2,48,4096]{2,1,0:T(8,128)(2,1)}), bf16[16,48,4096]{2,1,0:T(8,128)(2,1)}) %all-gather.6.cloned.1.call-update) | async-done | bytes 6291472 | tf_op jit(solution)/shard_map/all_gather | solution.py:257
  187.7 1.6 constant_dynamic-slice_fusion
  189.3 0.1 collective-permute-start
  189.4 3.4 %collective-permute-done = bf16[8,2,48,1024]{3,2,1,0:T(8,128)(2,1)S(1)} collective-permute-done((bf16[8,2,48,1024]{3,2,1,0:T(8,128)(2,1)S(1)}, bf16[8,2,48,1024]{3,2,1,0:T(8,128)(2,1)S(1)}, u32[]{:S(2)}, u32[]{:S(2)}) %collective-permute-start) | collective-permute-done | bytes 1572896 | tf_op jit(solution)/shard_map/ppermute | solution.py:262
  192.8 2.1 select_bitcast_fusion
  194.9 1.3 copy.11
  196.2 38.0 %elements.1 = f32[2,384,768]{2,1,0:T(8,128)} custom-call(bf16[2,2,1024,4096]{3,2,1,0:T(8,128)(2,1)} %w_ref.1, bf16[8,2,48,4096]{3,2,1,0:T(8,128)(2,1)} %bitcast.19, bf16[2,384,1024]{2,1,0:T(8,128)(2,1)} %bitcast.20), custom_call_target="tpu_custom_call" | custom-call | flops 25769803776 | bytes 33554432 | tf_op jit(solution)/shard_map/elements/pallas_call | solution.py:197
  234.2 1.8 convert_element_type.26
  235.9 0.1 copy.18
  236.0 32.2 %all_to_all.5 = bf16[16,2,24,768]{3,2,1,0:T(8,128)(2,1)S(1)} all-to-all(bf16[16,2,24,768]{3,2,1,0:T(8,128)(2,1)S(1)} %bitcast.16), channel_id=1, replica_groups=mesh['kpt'=2,'row'=8,'col'=2] {'row','col'}, dimensions={0} | all-to-all | bytes 2359296 | tf_op jit(solution)/shard_map/all_to_all | solution.py:272
  268.2 0.2 convert_reduce_fusion
  268.4 0.1 reshape.13
  268.5 0.7 copy.13
  (10 shorter events, 0.0 us)
Async XLA Ops:
  6.5 1.8 copy-start
  6.5 47.2 %all-gather.4.cloned.1.call-start = ((), (), s32[]{:S(2)}) async-start(), calls=%async_computation.1 | async-start | bytes 2228224 | tf_op jit(solution)/shard_map/all_gather | solution.py:240
  8.3 179.4 %all-gather.6.cloned.1.call-start = ((), (), s32[]{:S(2)}) async-start(), calls=%async_computation.2 | async-start | bytes 7077888 | tf_op jit(solution)/shard_map/all_gather | solution.py:257
  189.3 3.5 %collective-permute-start = (bf16[8,2,48,1024]{3,2,1,0:T(8,128)(2,1)S(1)}, bf16[8,2,48,1024]{3,2,1,0:T(8,128)(2,1)S(1)}, u32[]{:S(2)}, u32[]{:S(2)}) collective-permute-start(bf16[8,2,48,1024]{3,2,1,0:T(8,128)(2,1)S(1)} %constant_dynamic-slice_fusion), channel_id=1, source_target_pairs={{0,1},{1,0},{2,3},{3,2},{4,5},{5,4},{6,7},{7,6},{8,9},{9,8},{10,11... | collective-permute-start | bytes 4718600 | tf_op jit(solution)/shard_map/ppermute | solution.py:262
Sparse Core Ops, SparseCore 0:
  9.5 44.2 all-gather.3
  90.2 97.4 all-gather.5

commit v2 on v1

--- a/solution.py
+++ b/solution.py
@@ -7,6 +7,7 @@
 from jax.experimental import pallas as pl
 from jax.experimental.pallas import tpu as pltpu
 from jax.sharding import PartitionSpec as P
+
 
 IM = 64
 LANES = 128
@@ -161,21 +162,43 @@
     )(index, sel, grid, table, sign)
 
 
-def element_kernel(scale, w_ref, right_ref, left_ref, out_ref, right):
+def stack_pairs(right_ref, right):
     members, parts, owned, _ = right_ref.shape
     pairs = members * owned
-
-    @pl.when((pl.program_id(0) == 0) & (pl.program_id(1) == 0))
-    def _():
-        for r in range(members):
-            for c in range(parts):
-                right[c * pairs + r * owned : c * pairs + (r + 1) * owned, :] = right_ref[r, c]
-
+    for r in range(members):
+        for c in range(parts):
+            right[c * pairs + r * owned : c * pairs + (r + 1) * owned, :] = right_ref[r, c]
+
+
+def screened_terms(w_ref, right, pairs):
     nt = (((1,), (1,)), ((), ()))
     z_real = lax.dot_general(w_ref[0, 0], right[...], nt, preferred_element_type=jnp.float32)
     z_imag = lax.dot_general(w_ref[0, 1], right[...], nt, preferred_element_type=jnp.float32)
-    s_real = (z_real[:, :pairs] - z_imag[:, pairs:]) * scale
-    s_imag = (z_real[:, pairs:] + z_imag[:, :pairs]) * scale
+    return z_real[:, :pairs] - z_imag[:, pairs:], z_real[:, pairs:] + z_imag[:, :pairs]
+
+
+def first_kernel(w_ref, right_ref, out_ref, right):
+    pairs = right_ref.shape[0] * right_ref.shape[2]
+
+    @pl.when((pl.program_id(0) == 0) & (pl.program_id(1) == 0))
+    def _():
+        stack_pairs(right_ref, right)
+
+    s_real, s_imag = screened_terms(w_ref, right, pairs)
+    out_ref[0, :, :pairs] = s_real
+    out_ref[0, :, pairs:] = s_imag
+
+
+def element_kernel(scale, w_ref, right_ref, left_ref, first_ref, out_ref, right):
+    pairs = right_ref.shape[0] * right_ref.shape[2]
+
+    @pl.when((pl.program_id(0) == 0) & (pl.program_id(1) == 0))
+    def _():
+        stack_pairs(right_ref, right)
+
+    s_real, s_imag = screened_terms(w_ref, right, pairs)
+    s_real = (s_real + first_ref[0, :, :pairs]) * scale
+    s_imag = (s_imag + first_ref[0, :, pairs:]) * scale
     one = jnp.concatenate([s_real, s_imag], axis=1).astype(jnp.bfloat16)
     two = jnp.concatenate([s_imag, -s_real], axis=1).astype(jnp.bfloat16)
     got = jnp.dot(left_ref[0], one, preferred_element_type=jnp.float32)
@@ -190,29 +213,60 @@
         out_ref[0] += got
 
 
-def matrix_elements(screened, right, left, scale):
+def kernel_options(screened, right):
+    freqs, parts, rows, _ = screened.shape
+    width = right.shape[3]
+    pairs = right.shape[0] * right.shape[2]
+    return dict(
+        scratch_shapes=[pltpu.VMEM((parts * pairs, width), jnp.bfloat16)],
+        compiler_params=pltpu.CompilerParams(
+            dimension_semantics=("arbitrary", "arbitrary"), vmem_limit_bytes=60 * 1024 * 1024
+        ),
+        cost_estimate=pl.CostEstimate(
+            flops=8 * freqs * rows * width * pairs,
+            bytes_accessed=2 * freqs * parts * rows * width,
+            transcendentals=0,
+        ),
+    )
+
+
+def first_columns(screened, right):
+    freqs, parts, rows, _ = screened.shape
+    pairs, width = right.shape[0] * right.shape[2], right.shape[3]
+    tile = min(256, rows)
+    return pl.pallas_call(
+        first_kernel,
+        grid=(freqs, rows // tile),
+        out_shape=jax.ShapeDtypeStruct((freqs, rows, parts * pairs), jnp.float32),
+        in_specs=[
+            pl.BlockSpec((1, parts, tile, width), lambda f, i: (f, 0, i, 0)),
+            pl.BlockSpec(memory_space=pltpu.VMEM),
+        ],
+        out_specs=pl.BlockSpec((1, tile, parts * pairs), lambda f, i: (f, i, 0)),
+        name="first_columns",
+        **kernel_options(screened, right),
+    )(screened, right)
+
+
+def matrix_elements(screened, right, left, first, scale):
     freqs, parts, rows, columns = screened.shape
-    pairs = left.shape[1]
+    pairs, width = left.shape[1], right.shape[3]
     tile = min(256, rows)
+    last = columns // width - 1
     return pl.pallas_call(
         functools.partial(element_kernel, scale),
         grid=(freqs, rows // tile),
         out_shape=jax.ShapeDtypeStruct((freqs, pairs, parts * pairs), jnp.float32),
         in_specs=[
-            pl.BlockSpec((1, parts, tile, columns), lambda f, i: (f, 0, i, 0)),
+            pl.BlockSpec((1, parts, tile, width), lambda f, i: (f, 0, i, last)),
             pl.BlockSpec(memory_space=pltpu.VMEM),
             pl.BlockSpec((parts, pairs, tile), lambda f, i: (0, 0, i)),
+            pl.BlockSpec((1, tile, parts * pairs), lambda f, i: (f, i, 0)),
         ],
         out_specs=pl.BlockSpec((1, pairs, parts * pairs), lambda f, i: (f, 0, 0)),
-        scratch_shapes=[pltpu.VMEM((parts * pairs, columns), jnp.bfloat16)],
-        compiler_params=pltpu.CompilerParams(
-            dimension_semantics=("arbitrary", "arbitrary"), vmem_limit_bytes=60 * 1024 * 1024
-        ),
-        cost_estimate=pl.CostEstimate(
-            flops=8 * freqs * rows * columns * pairs, bytes_accessed=2 * screened.size, transcendentals=0
-        ),
         name="elements",
-    )(screened, right, left)
+        **kernel_options(screened, right),
+    )(screened, right, left, first)
 
 
 def plane_table(area):
@@ -254,16 +308,24 @@
     sign = jnp.where(far, -1.0, 1.0).astype(jnp.float32)[None, :]
 
     rho = pair_coefficients(grid, plane_table(area), sel, index, sign)[:, :owned]
-    right = lax.all_gather(rho, "row", axis=0, tiled=False)
+    cut = columns - columns // 4
+    early = lax.all_gather(rho[:, :, :cut], "row", axis=0, tiled=False)
+    late = lax.all_gather(rho[:, :, cut:], "row", axis=0, tiled=False)
+    first = first_columns(screened, early)
 
     start = row * row_span
-    block = lax.dynamic_slice_in_dim(right, start % columns, row_span, 3)
+    at = start % columns
+    block = jnp.where(
+        at < cut,
+        lax.dynamic_slice_in_dim(early, jnp.minimum(at, cut - row_span), row_span, 3),
+        lax.dynamic_slice_in_dim(late, jnp.maximum(at - cut, 0), row_span, 3),
+    )
     swap = [(i, (i + 1) % lax.axis_size("col")) for i in range(lax.axis_size("col"))]
     other = lax.ppermute(block, "col", swap)
     left = jnp.where(start // columns == col, block, other)
     left = jnp.swapaxes(left, 0, 1).reshape(2, count, row_span)
 
-    partial = matrix_elements(screened, right, left, 1.0 / math.sqrt(gmap.shape[0]))
+    partial = matrix_elements(screened, late, left, first, 1.0 / math.sqrt(gmap.shape[0]))
     freqs = partial.shape[0]
     devices = lax.axis_size(("row", "col"))
     share = count // devices

time: 276 us -> 304 us (1.10)
  waiting for transfers between devices: 109 us -> 129 us
  Pallas kernels: 74.2 us -> 79 us
    pallas_call x0 -> x1, Pallas kernels: none -> 26 us  [first_columns(): pl.pallas_call(first_kernel, grid=(freqs, rows // tile), out_shape=jax.Sh...]
    all_gather x1 -> x2, waiting for transfers between devices: 97.6 us -> 121 us  [the longest x1 79.9 us: shards(): early = lax.all_gather(rho[:, :, :cut], 'row', axis=0, tiled=False)]
    pallas_call x1, Pallas kernels: 38 us -> 16.7 us  [matrix_elements(): pl.pallas_call(functools.partial(element_kernel, scale), grid=(freqs, row...]
    slice x0 -> x2, local copies, waits for them, and re-layouts: none -> 3.56 us  [the longest x1 1.93 us: shards(): early = lax.all_gather(rho[:, :, :cut], 'row', axis=0, tiled=False)]
    ppermute x1, waiting for transfers between devices: 3.38 us -> 0.01 us  [shards(): other = lax.ppermute(block, 'col', swap)]
  transfers between devices with their start and end apart: 3 -> 4, of which waited for: 3 -> 3; matrix products, arithmetic and copies ran while one was open for 14% -> 13% of each run, Pallas kernels for 0% -> 9%
where the time goes in v2:
time: 304 us
  waiting for transfers between devices  129 us (42%)
  Pallas kernels  79 us (26%)
  other arithmetic  42 us (14%)
  blocking collectives  32.8 us (11%)
  between operations  13.2 us (4%)
  local copies, waits for them, and re-layouts  7.57 us (2%)
    all_gather x1, waiting for transfers between devices, shards(): early = lax.all_gather(rho[:, :, :cut], 'row', axis=0, tiled=False)  79.9 us
    all_gather x1, waiting for transfers between devices, shards(): late = lax.all_gather(rho[:, :, cut:], 'row', axis=0, tiled=False)  41 us
    pallas_call x1, Pallas kernels, pair_coefficients(): pl.pallas_call(functools.partial(rho_kernel, norm), out_shape=jax.ShapeDt...  36.3 us
    convert_element_type x1, other arithmetic, plane_table(): jnp.cos(turn.astype(jnp.float32) * (2.0 * math.pi / side))  34 us
    all_to_all x1, blocking collectives, shards(): lax.all_to_all(pieces, ('row', 'col'), split_axis=0, concat_axis=0, tiled...  32.8 us
    pallas_call x1, Pallas kernels, first_columns(): pl.pallas_call(first_kernel, grid=(freqs, rows // tile), out_shape=jax.Sh...  26 us
    pallas_call x1, Pallas kernels, matrix_elements(): pl.pallas_call(functools.partial(element_kernel, scale), grid=(freqs, row...  16.7 us
    all_gather x1, waiting for transfers between devices, shards(): grid = lax.all_gather(local, ('row', 'col'), axis=0, tiled=True)  7.87 us
  transfers between devices with their start and end apart: 4, of which 3 were waited for; matrix products, arithmetic and copies ran while one was open for 13% of the time, Pallas kernels for 9%

profile of v2, /device:TPU:0, one launch (start us, length us, event | category | flops | bytes accessed | tf_op | source)
XLA Modules:
  0.0 303.6 jit_solution(11624831698760620273)
XLA Ops:
  6.5 1.7 copy.19
  8.3 0.1 dynamic-slice_bitcast_fusion
  8.4 0.1 eq.30
  8.5 1.3 compare_select_fusion
  9.9 1.4 fusion.18.index_ref
  11.2 0.7 fusion.14.sel_ref
  11.9 34.0 %fusion.8.table_ref = bf16[1024,2048]{1,0:T(8,128)(2,1)} fusion(s32[2048]{0:T(1024)S(1)} %fusion.32, s32[1024]{0:T(1024)S(1)} %get-tuple-element.10, s32[1024]{0:T(1024)S(1)} %get-tuple-element.11, s32[2048]{0:T(1024)S(1)} %get-tuple-element.7, s32[2048]{0:T(1024)S(1)} %get-tuple-element.8, s32[1024]{0:T(1024)S(1)} %get-tuple-element.9, ...), kind=kLoop, calls=%fused_computation.19 | loop fusion | flops 83886080 | bytes 4239360 | tf_op jit(solution)/shard_map/convert_element_type | solution.py:279
  45.9 7.9 %all-gather.6.cloned.1.call-done.grid_ref = bf16[32,32,1024]{2,1,0:T(8,128)(2,1)} async-done(((bf16[2,32,1024]{2,1,0:T(8,128)(2,1)}), bf16[32,32,1024]{2,1,0:T(8,128)(2,1)}) %all-gather.6.cloned.1.call-update) | async-done | bytes 2097168 | tf_op jit(solution)/shard_map/all_gather | solution.py:294
  53.8 36.3 %rho.1 = bf16[2,48,4096]{2,1,0:T(8,128)(2,1)} custom-call(s32[4096]{0:T(1024)} %fusion.18.index_ref, bf16[96,32]{1,0:T(8,128)(2,1)} %fusion.14.sel_ref, bf16[32,32,1024]{2,1,0:T(8,128)(2,1)} %all-gather.6.cloned.1.call-done.grid_ref, bf16[1024,2048]{1,0:T(8,128)(2,1)} %fusion.8.table_ref, f32[1,4096]{1,0:T(1,128)} %bitcast.25), custom_call_target="tpu_custom_call" | custom-call | flops 10000000000 | bytes 8388608 | tf_op jit(solution)/shard_map/rho/pallas_call | solution.py:148
  90.1 1.6 slice.8
  91.8 1.9 slice.9
  93.8 41.0 %all-gather.8.cloned.1.call-done = bf16[16,48,1024]{2,1,0:T(8,128)(2,1)} async-done(((bf16[2,48,1024]{2,1,0:T(8,128)(2,1)}), bf16[16,48,1024]{2,1,0:T(8,128)(2,1)}) %all-gather.8.cloned.1.call-update) | async-done | bytes 1572880 | tf_op jit(solution)/shard_map/all_gather | solution.py:313
  134.8 79.9 %all-gather.10.cloned.1.call-done = bf16[16,48,3072]{2,1,0:T(8,128)(2,1)} async-done(((bf16[2,48,3072]{2,1,0:T(8,128)(2,1)}), bf16[16,48,3072]{2,1,0:T(8,128)(2,1)}) %all-gather.10.cloned.1.call-update) | async-done | bytes 4718608 | tf_op jit(solution)/shard_map/all_gather | solution.py:312
  214.7 2.5 dynamic-slice_select_fusion
  217.3 26.0 %first_columns.1.first_ref = f32[2,1024,768]{2,1,0:T(8,128)} custom-call(bf16[2,2,1024,4096]{3,2,1,0:T(8,128)(2,1)} %w_ref.3, bf16[8,2,48,3072]{3,2,1,0:T(8,128)(2,1)} %bitcast.23), custom_call_target="tpu_custom_call" | custom-call | flops 19327352832 | bytes 25165824 | tf_op jit(solution)/shard_map/first_columns/pallas_call | solution.py:237
  243.2 0.2 select_bitcast_fusion
  243.4 1.3 copy.11
  244.7 16.7 %elements.1 = f32[2,384,768]{2,1,0:T(8,128)} custom-call(bf16[2,2,1024,4096]{3,2,1,0:T(8,128)(2,1)} %w_ref.3, bf16[8,2,48,1024]{3,2,1,0:T(8,128)(2,1)} %bitcast.17, bf16[2,384,1024]{2,1,0:T(8,128)(2,1)} %bitcast.18, f32[2,1024,768]{2,1,0:T(8,128)} %first_columns.1.first_ref), custom_call_target="tpu_custom_call" | custom-call | flops 6442450944 | bytes 8388608 | tf_op jit(solution)/shard_map/elements/pallas_call | solution.py:256
  261.5 1.8 convert_element_type.26
  263.3 0.1 copy.18
  263.3 32.8 %all_to_all.5 = bf16[16,2,24,768]{3,2,1,0:T(8,128)(2,1)S(1)} all-to-all(bf16[16,2,24,768]{3,2,1,0:T(8,128)(2,1)S(1)} %bitcast.20), channel_id=1, replica_groups=mesh['kpt'=2,'row'=8,'col'=2] {'row','col'}, dimensions={0} | all-to-all | bytes 2359296 | tf_op jit(solution)/shard_map/all_to_all | solution.py:334
  296.2 0.2 convert_reduce_fusion
  296.3 0.1 reshape.13
  296.4 0.7 copy.13
  (18 shorter events, 0.2 us)
Async XLA Ops:
  6.5 1.8 copy-start
  6.5 47.3 %all-gather.6.cloned.1.call-start = ((), (), s32[]{:S(2)}) async-start(), calls=%async_computation.1 | async-start | bytes 2228224 | tf_op jit(solution)/shard_map/all_gather | solution.py:294
  8.3 126.6 %all-gather.8.cloned.1.call-start = ((), (), s32[]{:S(2)}) async-start(), calls=%async_computation.2 | async-start | bytes 1769472 | tf_op jit(solution)/shard_map/all_gather | solution.py:313
  91.7 123.0 %all-gather.10.cloned.1.call-start = ((), (), s32[]{:S(2)}) async-start(), calls=%async_computation.3 | async-start | bytes 5308416 | tf_op jit(solution)/shard_map/all_gather | solution.py:312
  217.2 26.0 %collective-permute-start = (bf16[8,2,48,1024]{3,2,1,0:T(8,128)(2,1)S(1)}, bf16[8,2,48,1024]{3,2,1,0:T(8,128)(2,1)S(1)}, u32[]{:S(2)}, u32[]{:S(2)}) collective-permute-start(bf16[8,2,48,1024]{3,2,1,0:T(8,128)(2,1)S(1)} %dynamic-slice_select_fusion), channel_id=1, source_target_pairs={{0,1},{1,0},{2,3},{3,2},{4,5},{5,4},{6,7},{7,6},{8,9},{9,8},{10,11... | collective-permute-start | bytes 4718600 | tf_op jit(solution)/shard_map/ppermute | solution.py:324
  244.7 52.4 %copy-start.1 = (s32[384,2]{0,1:T(2,128)S(1)}, s32[384,2]{0,1:T(2,128)}, u32[]{:S(2)}) copy-start(s32[384,2]{0,1:T(2,128)} %param.5) | copy-start | bytes 9220
Sparse Core Ops, SparseCore 0:
  9.5 44.2 all-gather.5
  91.9 42.9 all-gather.7
  137.0 77.6 all-gather.9
